TPU v7x, 32 devices: a whole 2x2x4 slice. The times are simulated.
32 devices in a mesh: grp: 2 (over y), gx: 4 (over z), gy: 4 (over x, core).
Axes of the slice: x: 2, y: 2, z: 4, core: 2. Of those that a mesh axis runs over, the one named last changes fastest.
Arguments:
- samples: bfloat16 [2816, 65536], P('grp', ('gx', 'gy')), parts along dimension 0, may hold values from -400 to 400
- tile_owner: int32 [256], replicated, may hold values from 0 to 255, each once
Outputs:
- kernel_tiles: float32 [512, 4096], P(('grp', 'gx', 'gy')), parts along dimension 0
There are 2 independent parts, one for each index of `grp`. A program takes and returns all parts, laid end to end along the dimension named above; an argument that names none is the same for every part. Nothing has to cross between parts.
Inputs may be any that keep to these rules, and one draw needn't show every extreme that they name: tile_owner holds each of 0 to 255 once; device k of the group (k = gx index * 4 + gy index) owns slots k * 16 to (k + 1) * 16 - 1; values of 253 and above mark empty slots.
All inputs are finite; a program needn't handle non-finite values.
Results may differ from a plain program's by a relative error of at most 0.0003.
Values sent between devices are 32-bit elements; how exact they have to be, the bound alone decides.
No kernel may reach another device: no remote copies, remote signals or barrier semaphores. Data moves between devices by JAX's collectives and lax.ppermute only.
A program may use at most 64 MiB of HBM per device.

v0:
```python
import functools

import jax
import jax.numpy as jnp
from jax import lax
from jax.experimental import pallas as pl
from jax.experimental.pallas import tpu as pltpu
from jax.sharding import PartitionSpec as P


TILE = 64
HALF = TILE // 2
LANES = 2 * TILE
PITCH = HALF + 8
EPS = 1e-06
AXES = ("gx", "gy")


def row_cuts(rows):
    cuts = list(range(0, rows, 256))
    if len(cuts) > 1 and rows - cuts[-1] < 256:
        cuts.pop()
    return tuple(zip(cuts, cuts[1:] + [rows]))


def gram_kernel(cuts, spans, hbm_ref, tiles, squares, x_ref, g_ref, sems):
    copies = [
        pltpu.make_async_copy(hbm_ref.at[:, pl.ds(lo, hi - lo)], x_ref.at[:, pl.ds(lo, hi - lo)], sems.at[n])
        for n, (lo, hi) in enumerate(spans)
    ]
    for copy in copies:
        copy.start()
    left = lax.broadcasted_iota(jnp.int32, (HALF, LANES), 1) < TILE
    eye = lax.broadcasted_iota(jnp.int32, (LANES, LANES), 0) == lax.broadcasted_iota(jnp.int32, (LANES, LANES), 1)
    diagonal = []
    for n, (k0, k1) in enumerate(spans):
        copies[n].wait()
        for m, (r0, r1) in enumerate(cuts):
            for c0, c1 in cuts[: m + 1]:
                block = lax.dot_general(
                    x_ref[r0:r1, k0:k1], x_ref[c0:c1, k0:k1], (((1,), (1,)), ((), ())), preferred_element_type=jnp.float32
                )
                if n:
                    block = g_ref[r0:r1, c0:c1] + block
                g_ref[r0:r1, c0:c1] = block
                if n + 1 < len(spans):
                    continue
                for row in range(r0 // TILE, r1 // TILE):
                    for b in range(c0 // LANES, c1 // LANES):
                        col = 2 * b
                        if col > row:
                            continue
                        lanes = slice(b * LANES, (b + 1) * LANES)
                        upper = g_ref[row * TILE : row * TILE + HALF, lanes]
                        lower = g_ref[row * TILE + HALF : (row + 1) * TILE, lanes]
                        at = (row * (row + 1) // 2 + col) * HALF
                        tiles[at : at + HALF, :] = jnp.where(left, upper, pltpu.roll(lower, TILE, 1))
                        if col + 1 <= row:
                            tiles[at + HALF : at + 2 * HALF, :] = jnp.where(left, pltpu.roll(upper, TILE, 1), lower)
            if n + 1 == len(spans):
                for b in range(r0 // LANES, r1 // LANES):
                    part = g_ref[b * LANES : (b + 1) * LANES, b * LANES : (b + 1) * LANES]
                    diagonal.append(jnp.sum(jnp.where(eye, part, 0.0), axis=0, keepdims=True))
    high = cuts[-1][1] // TILE
    live = high * (high + 1) // 2 * HALF
    tiles[live:, :] = jnp.zeros((tiles.shape[0] - live, LANES), jnp.float32)
    extra = squares.shape[0]
    squares[...] = jnp.concatenate(diagonal + [jnp.zeros((extra - len(diagonal), LANES), jnp.float32)], axis=0)


def gram_tiles(samples, count, extra):
    rows, features = samples.shape
    cuts = row_cuts(rows)
    first = features // 4
    spans = ((0, first), (first, features)) if first % LANES == 0 else ((0, features),)
    vmem = pl.BlockSpec(memory_space=pltpu.VMEM)
    return pl.pallas_call(
        functools.partial(gram_kernel, cuts, spans),
        out_shape=[
            jax.ShapeDtypeStruct((count * HALF, LANES), jnp.float32),
            jax.ShapeDtypeStruct((extra, LANES), jnp.float32),
        ],
        in_specs=[pl.BlockSpec(memory_space=pltpu.HBM)],
        out_specs=[vmem] * 2,
        scratch_shapes=[
            pltpu.VMEM((rows, features), samples.dtype),
            pltpu.VMEM((rows, rows), jnp.float32),
            pltpu.SemaphoreType.DMA((len(spans),)),
        ],
        compiler_params=pltpu.CompilerParams(vmem_limit_bytes=44 * 2**20),
        cost_estimate=pl.CostEstimate(
            flops=rows * rows * features, bytes_accessed=rows * features * 2 + count * HALF * LANES * 4, transcendentals=0
        ),
        name="gram_tiles",
    )(samples)


def pick_kernel(pieces, bounds, columns, slots, owner_ref, tiles, squares, *outs):
    at_x, at_y = lax.axis_index("gx"), lax.axis_index("gy")
    for out, atoms in zip(outs, pieces):
        at = 0
        for far_x, far_y, k in atoms:
            dest = (at_x ^ far_x) * columns + (at_y ^ far_y)
            lo, hi = bounds[k]
            for i in range(lo // HALF, min(hi // HALF, slots)):
                source = pl.multiple_of(owner_ref[dest * slots + i] * HALF, HALF)
                out[at : at + HALF, :] = tiles[pl.ds(source, HALF), :]
                at += HALF
            if hi == bounds[-1][1]:
                out[at : at + squares.shape[0], :] = squares[...]
                at += squares.shape[0]


def pick_tiles(owner, tiles, squares, pieces, bounds, columns, slots):
    sizes = [sum(bounds[k][1] - bounds[k][0] for _, _, k in atoms) for atoms in pieces]
    vmem, smem = pl.BlockSpec(memory_space=pltpu.VMEM), pl.BlockSpec(memory_space=pltpu.SMEM)
    return pl.pallas_call(
        functools.partial(pick_kernel, pieces, bounds, columns, slots),
        out_shape=[jax.ShapeDtypeStruct((size, LANES), jnp.float32) for size in sizes],
        in_specs=[smem, vmem, vmem],
        out_specs=[vmem] * len(sizes),
        compiler_params=pltpu.CompilerParams(vmem_limit_bytes=2**20),
        cost_estimate=pl.CostEstimate(flops=10**6, bytes_accessed=sum(sizes) * LANES * 8, transcendentals=0),
        name="pick_tiles",
    )(owner, tiles, squares)


def finish_kernel(joined, slots, features, index_ref, *refs):
    out_ref, total, inv, rows_of, cols_of, packed = refs[-6:]
    add_kernel(joined, *refs[:-6], total)
    meansq = total[slots * HALF :, :] / features + EPS
    inv[...] = 1.0 / jnp.sqrt(meansq)
    half = lax.broadcasted_iota(jnp.int32, (1, LANES), 1) < TILE

    def pick(tile):
        line = inv[pl.ds(lax.div(tile, 2), 1), :]
        turned = pltpu.roll(line, TILE, 1)
        odd = lax.rem(tile, 2) == 1
        return jnp.where(odd, turned, line), jnp.where(odd, line, turned)

    rows_of[...] = jnp.zeros_like(rows_of)
    for i in range(slots):
        first, second = pick(index_ref[i])
        rows_of[i : i + 1, :] = first
        first, second = pick(index_ref[slots + i])
        alive = index_ref[2 * slots + i] == 1
        cols_of[i : i + 1, :] = jnp.where(half, first, second)
    down = rows_of[...].T
    left = lax.broadcasted_iota(jnp.int32, (HALF, LANES), 1) < TILE
    norm = 1.0 / features**0.5
    for i in range(slots):
        by_row = jnp.where(left, down[:HALF, i : i + 1], down[HALF:TILE, i : i + 1])
        scaled = total[i * HALF : (i + 1) * HALF, :] * by_row * (cols_of[i : i + 1, :] * norm)
        alive = index_ref[2 * slots + i] == 1
        packed[i * PITCH : i * PITCH + HALF, :] = jnp.where(alive, scaled, 0.0)
    step = min(slots, 8)
    wide = lax.broadcasted_iota(jnp.int32, (step, LANES), 1) < TILE
    for s in range(0, slots, step):
        for j in range(HALF):
            q = (2 * j) % HALF
            even = packed[pl.ds(s * PITCH + q, step, stride=PITCH), :]
            odd = packed[pl.ds(s * PITCH + q + 1, step, stride=PITCH), :]
            if 2 * j < HALF:
                line = jnp.where(wide, even, pltpu.roll(odd, TILE, 1))
            else:
                line = jnp.where(wide, pltpu.roll(even, TILE, 1), odd)
            out_ref[s : s + step, j * LANES : (j + 1) * LANES] = line


def finish(index, arrays, joined, slots, features):
    per = sum(size for _, size in joined)
    extra = per - slots * HALF
    vmem = pl.BlockSpec(memory_space=pltpu.VMEM)
    return pl.pallas_call(
        functools.partial(finish_kernel, joined, slots, features),
        out_shape=jax.ShapeDtypeStruct((slots, TILE * TILE), jnp.float32),
        in_specs=[pl.BlockSpec(memory_space=pltpu.SMEM)] + [vmem] * len(arrays),
        out_specs=vmem,
        scratch_shapes=[
            pltpu.VMEM((per, LANES), jnp.float32),
            pltpu.VMEM((extra, LANES), jnp.float32),
            pltpu.VMEM((LANES, LANES), jnp.float32),
            pltpu.VMEM((max(slots, 8), LANES), jnp.float32),
            pltpu.VMEM((slots * PITCH, LANES), jnp.float32),
        ],
        compiler_params=pltpu.CompilerParams(vmem_limit_bytes=6 * 2**20),
        cost_estimate=pl.CostEstimate(flops=per * LANES * 8, bytes_accessed=per * LANES * 32, transcendentals=0),
        name="finish_tiles",
    )(index, *arrays)


def add_kernel(joined, *refs):
    at = 0
    for parts, size in joined:
        value = refs[parts[0][0]][parts[0][1] : parts[0][1] + size, :]
        for i, lo in parts[1:]:
            value = value + refs[i][lo : lo + size, :]
        refs[-1][at : at + size, :] = value
        at += size


def add_terms(arrays, joined):
    rows = sum(size for _, size in joined)
    vmem = pl.BlockSpec(memory_space=pltpu.VMEM)
    return pl.pallas_call(
        functools.partial(add_kernel, joined),
        out_shape=jax.ShapeDtypeStruct((rows, LANES), jnp.float32),
        in_specs=[vmem] * len(arrays),
        out_specs=vmem,
        compiler_params=pltpu.CompilerParams(vmem_limit_bytes=2 * 2**20),
        cost_estimate=pl.CostEstimate(flops=rows * LANES * 3, bytes_accessed=rows * LANES * 16, transcendentals=0),
        name="add_terms",
    )(*arrays)


def index_kernel(slots, columns, firsts, owner_ref, out_ref):
    at = (lax.axis_index("gx") * columns + lax.axis_index("gy")) * slots
    for i in range(slots):
        tile = owner_ref[at + i]
        row = jnp.int32(0)
        for first in firsts[1:-1]:
            row = row + (tile >= first).astype(jnp.int32)
        alive = tile < firsts[-1]
        out_ref[i] = jnp.where(alive, row, 0)
        out_ref[slots + i] = jnp.where(alive, tile - row * (row + 1) // 2, 0)
        out_ref[2 * slots + i] = alive.astype(jnp.int32)


def tile_index(owner, slots, columns, side):
    smem = pl.BlockSpec(memory_space=pltpu.SMEM)
    firsts = tuple(k * (k + 1) // 2 for k in range(side + 1))
    return pl.pallas_call(
        functools.partial(index_kernel, slots, columns, firsts),
        out_shape=jax.ShapeDtypeStruct((3 * slots,), jnp.int32),
        in_specs=[smem],
        out_specs=smem,
        compiler_params=pltpu.CompilerParams(vmem_limit_bytes=2**20),
        cost_estimate=pl.CostEstimate(flops=10**6, bytes_accessed=2**10, transcendentals=0),
        name="tile_index",
    )(owner)


def cut(per, parts):
    total = sum(parts)
    marks = [0]
    for part in parts:
        marks.append(marks[-1] + part)
    marks = [mark * per // total // HALF * HALF for mark in marks[:-1]] + [per]
    return list(zip(marks, marks[1:]))


def halving(gx, gy, per):
    bounds = cut(per, [1])
    blocks = [(x, y, 0) for y in range(gy) for x in range(gx)]
    pieces, sends = [], []
    for axis, size in (("gy", gy), ("gx", gx)):
        for bit in (1 << b for b in range(size.bit_length() - 1)):
            far = [block for block in blocks if (block[1] if axis == "gy" else block[0]) & bit]
            blocks = [block for block in blocks if block not in far]
            pieces = pieces or [(0, [far]), (1, [blocks])]
            sends.append((axis, bit, far))
    return bounds, pieces, sends


def plan(gx, gy, per):
    if (gx, gy) != (4, 4):
        return halving(gx, gy, per)
    core, x, z, zz = ("gy", 1), ("gy", 2), ("gx", 1), ("gx", 2)
    bounds = cut(per, [1, 3])
    sent = [
        [(3, 3, 1)],
        [(3, 3, 0), (1, 3, 0), (3, 1, 0), (1, 1, 0)],
        [(2, 3, 1)],
        [(1, 3, 1), (0, 3, 1)],
        [(2, 3, 0), (2, 1, 0), (0, 3, 0), (0, 1, 0)],
        [(r, 1, 1) for r in range(4)],
    ]
    kept = [[(r, y & 2, k) for r, y, k in atoms] for atoms in sent]
    groups = [(0, sent), (2, kept)]
    first, second, *others = [(*core, atoms) for atoms in sent]
    sends = [first, second, (*x, [(3, 2, 1)]), (*z, [(3, 2, 0), (1, 2, 0), (3, 0, 0), (1, 0, 0)]), *others]
    sends += [(*x, [(r, 2, 1)]) for r in (2, 1, 0)]
    sends += [(*z, [(3, 0, 1)]), (*zz, [(2, 2, 0), (2, 0, 0)]), (*zz, [(2, 0, 1)]), (*z, [(1, 0, 1)]), (*x, [(0, 2, 0)])]
    return bounds, groups, sends


def shards(mesh, samples, owner):
    gx, gy = mesh.shape["gx"], mesh.shape["gy"]
    slots = owner.shape[0] // (gx * gy)
    rows = samples.shape[0]
    features = samples.shape[1] * gx * gy
    extra = -(-(rows // LANES) // 8) * 8
    per = slots * HALF + extra
    bounds, groups, sends = plan(gx, gy, per)
    pieces = [atoms for _, group in groups for atoms in group]

    def pairs(axis, bit):
        if axis == "gx":
            return [(i * gy + j, (i ^ bit) * gy + j) for i in range(gx) for j in range(gy)]
        return [(i * gy + j, i * gy + (j ^ bit)) for i in range(gx) for j in range(gy)]

    tiles, squares = gram_tiles(samples, owner.shape[0], extra)
    pick = functools.partial(
        pick_tiles, owner, tiles, squares, bounds=bounds, columns=gy, slots=slots
    )
    arrays = []
    for _, group in groups:
        arrays += pick(pieces=group)
    index = tile_index(owner, slots, gy, rows // TILE)
    terms = {}
    for n, atoms in enumerate(pieces):
        at = 0
        for atom in atoms:
            terms[atom] = [(n, at)]
            at += bounds[atom[2]][1] - bounds[atom[2]][0]

    def runs(atoms):
        joined = []
        for atom in atoms:
            size = bounds[atom[2]][1] - bounds[atom[2]][0]
            mine = terms.pop(atom)
            if joined and [(i, lo - joined[-1][1]) for i, lo in mine] == joined[-1][0]:
                joined[-1][1] += size
            else:
                joined.append([list(mine), size])
        return joined

    def gather(joined):
        used = sorted({i for parts, _ in joined for i, _ in parts})
        local = {i: k for k, i in enumerate(used)}
        return [arrays[i] for i in used], tuple(
            (tuple((local[i], lo) for i, lo in parts), size) for parts, size in joined
        )

    for axis, bit, atoms in sends:
        values, joined = gather(runs(atoms))
        if len(values) == 1 and len(joined) == 1 and values[0].shape[0] == joined[0][1]:
            sent = values[0]
        else:
            sent = add_terms(values, joined)
        arrays.append(lax.ppermute(sent, AXES, pairs(axis, bit)))
        at = 0
        for x, y, k in atoms:
            there = (x & ~bit, y, k) if axis == "gx" else (x, y & ~bit, k)
            terms[there].append((len(arrays) - 1, at))
            at += bounds[k][1] - bounds[k][0]
    values, joined = gather(runs([(0, 0, k) for k in range(len(bounds))]))
    assert not terms
    return finish(index, values, joined, slots, features)


def solution(mesh):
    step = jax.shard_map(
        functools.partial(shards, mesh),
        mesh=mesh,
        in_specs=(P("grp", AXES), P()),
        out_specs=P(("grp", "gx", "gy"), None),
        check_vma=False,
    )
    _, _, _ = plan(mesh.shape["gx"], mesh.shape["gy"], 1024)
    return step
```

profile of v0, /device:TPU:0, one launch (start us, length us, event | category | flops | bytes accessed | tf_op | source)
XLA Modules:
  0.0 58.9 jit_solution(18105370162844477515)
XLA Ops:
  0.0 12.6 %gram_tiles.1 = (f32[8192,128]{1,0:T(8,128)S(1)}, f32[16,128]{1,0:T(8,128)S(1)}) custom-call(bf16[1408,4096]{1,0:T(8,128)(2,1)} %hbm_ref.1), custom_call_target="tpu_custom_call" | custom-call | flops 8120172544 | bytes 15728640 | tf_op jit(solution)/shard_map/gram_tiles/pallas_call | solution.py:77
  12.6 0.7 %pick_tiles.3 = (f32[400,128]{1,0:T(8,128)S(1)}, f32[512,128]{1,0:T(8,128)S(1)}, f32[400,128]{1,0:T(8,128)S(1)}, f32[800,128]{1,0:T(8,128)S(1)}, f32[512,128]{1,0:T(8,128)S(1)}, /*index=5*/f32[1600,128]{1,0:T(8,128)S(1)}) custom-call(s32[256]{0:T(256)S(1)} %copy-done, f32[8192,128]{1,0:T(8,128)S(1)} %get-tuple-element.19.tiles, ...), custom_call_target="tpu_custom_call" | custom-call | flops 1000000 | bytes 4325376 | tf_op jit(solution)/shard_map/pick_tiles/pallas_call | solution.py:117
  13.3 0.6 collective-permute-start.3
  14.0 0.4 collective-permute-start.9
  14.5 0.4 collective-permute-start.7
  14.9 0.7 %pick_tiles.2 = (f32[400,128]{1,0:T(8,128)S(1)}, f32[512,128]{1,0:T(8,128)S(1)}, f32[400,128]{1,0:T(8,128)S(1)}, f32[800,128]{1,0:T(8,128)S(1)}, f32[512,128]{1,0:T(8,128)S(1)}, /*index=5*/f32[1600,128]{1,0:T(8,128)S(1)}) custom-call(s32[256]{0:T(256)S(1)} %copy-done, f32[8192,128]{1,0:T(8,128)S(1)} %get-tuple-element.19.tiles, ...), custom_call_target="tpu_custom_call" | custom-call | flops 1000000 | bytes 4325376 | tf_op jit(solution)/shard_map/pick_tiles/pallas_call | solution.py:117
  15.6 1.1 %collective-permute-done.9.refs_1_ = f32[400,128]{1,0:T(8,128)S(1)} collective-permute-done((f32[400,128]{1,0:T(8,128)S(1)}, f32[400,128]{1,0:T(8,128)S(1)}, u32[]{:S(2)}, u32[]{:S(2)}) %collective-permute-start.9) | collective-permute-done | bytes 204832 | tf_op jit(solution)/shard_map/ppermute | solution.py:341
  16.8 2.9 %collective-permute-start.10 = (f32[400,128]{1,0:T(8,128)S(1)}, f32[400,128]{1,0:T(8,128)S(1)}, u32[]{:S(2)}, u32[]{:S(2)}) collective-permute-start(f32[400,128]{1,0:T(8,128)S(1)} %add_terms.14), channel_id=1, source_target_pairs={{0,2},{1,3},{2,0},{3,1},{4,6},{5,7},{6,4},{7,5},{8,10},{9,11},{10,... | collective-permute-start | bytes 614408 | tf_op jit(solution)/shard_map/ppermute | solution.py:341
  19.7 1.6 %collective-permute-start.1 = (f32[512,128]{1,0:T(8,128)S(1)}, f32[512,128]{1,0:T(8,128)S(1)}, u32[]{:S(2)}, u32[]{:S(2)}) collective-permute-start(f32[512,128]{1,0:T(8,128)S(1)} %add_terms.10), channel_id=1, source_target_pairs={{0,4},{1,5},{2,6},{3,7},{4,0},{5,1},{6,2},{7,3},{8,12},{9,13},{10,... | collective-permute-start | bytes 786440 | tf_op jit(solution)/shard_map/ppermute | solution.py:341
  21.4 0.6 %collective-permute-start.13 = (f32[400,128]{1,0:T(8,128)S(1)}, f32[400,128]{1,0:T(8,128)S(1)}, u32[]{:S(2)}, u32[]{:S(2)}) collective-permute-start(f32[400,128]{1,0:T(8,128)S(1)} %add_terms.17), channel_id=1, source_target_pairs={{0,2},{1,3},{2,0},{3,1},{4,6},{5,7},{6,4},{7,5},{8,10},{9,11},{10,... | collective-permute-start | bytes 614408 | tf_op jit(solution)/shard_map/ppermute | solution.py:341
  22.0 3.6 %collective-permute-done.10.refs_1_ = f32[400,128]{1,0:T(8,128)S(1)} collective-permute-done((f32[400,128]{1,0:T(8,128)S(1)}, f32[400,128]{1,0:T(8,128)S(1)}, u32[]{:S(2)}, u32[]{:S(2)}) %collective-permute-start.10) | collective-permute-done | bytes 204832 | tf_op jit(solution)/shard_map/ppermute | solution.py:341
  25.6 2.0 %collective-permute-start.8 = (f32[400,128]{1,0:T(8,128)S(1)}, f32[400,128]{1,0:T(8,128)S(1)}, u32[]{:S(2)}, u32[]{:S(2)}) collective-permute-start(f32[400,128]{1,0:T(8,128)S(1)} %add_terms.13), channel_id=1, source_target_pairs={{0,2},{1,3},{2,0},{3,1},{4,6},{5,7},{6,4},{7,5},{8,10},{9,11},{10,... | collective-permute-start | bytes 614408 | tf_op jit(solution)/shard_map/ppermute | solution.py:341
  27.7 1.6 %collective-permute-start.11 = (f32[400,128]{1,0:T(8,128)S(1)}, f32[400,128]{1,0:T(8,128)S(1)}, u32[]{:S(2)}, u32[]{:S(2)}) collective-permute-start(f32[400,128]{1,0:T(8,128)S(1)} %add_terms.15), channel_id=1, source_target_pairs={{0,4},{1,5},{2,6},{3,7},{4,0},{5,1},{6,2},{7,3},{8,12},{9,13},{10,... | collective-permute-start | bytes 614408 | tf_op jit(solution)/shard_map/ppermute | solution.py:341
  29.3 0.6 %collective-permute-done.13.refs_2_ = f32[400,128]{1,0:T(8,128)S(1)} collective-permute-done((f32[400,128]{1,0:T(8,128)S(1)}, f32[400,128]{1,0:T(8,128)S(1)}, u32[]{:S(2)}, u32[]{:S(2)}) %collective-permute-start.13) | collective-permute-done | bytes 204832 | tf_op jit(solution)/shard_map/ppermute | solution.py:341
  30.0 2.0 %collective-permute-start.5 = (f32[400,128]{1,0:T(8,128)S(1)}, f32[400,128]{1,0:T(8,128)S(1)}, u32[]{:S(2)}, u32[]{:S(2)}) collective-permute-start(f32[400,128]{1,0:T(8,128)S(1)} %add_terms.11), channel_id=1, source_target_pairs={{0,2},{1,3},{2,0},{3,1},{4,6},{5,7},{6,4},{7,5},{8,10},{9,11},{10,... | collective-permute-start | bytes 614408 | tf_op jit(solution)/shard_map/ppermute | solution.py:341
  32.0 2.3 %collective-permute-done.8.refs_2_ = f32[400,128]{1,0:T(8,128)S(1)} collective-permute-done((f32[400,128]{1,0:T(8,128)S(1)}, f32[400,128]{1,0:T(8,128)S(1)}, u32[]{:S(2)}, u32[]{:S(2)}) %collective-permute-start.8) | collective-permute-done | bytes 204832 | tf_op jit(solution)/shard_map/ppermute | solution.py:341
  34.4 2.1 %collective-permute-start.14 = (f32[400,128]{1,0:T(8,128)S(1)}, f32[400,128]{1,0:T(8,128)S(1)}, u32[]{:S(2)}, u32[]{:S(2)}) collective-permute-start(f32[400,128]{1,0:T(8,128)S(1)} %add_terms.18), channel_id=1, source_target_pairs={{0,4},{1,5},{2,6},{3,7},{4,0},{5,1},{6,2},{7,3},{8,12},{9,13},{10,... | collective-permute-start | bytes 614408 | tf_op jit(solution)/shard_map/ppermute | solution.py:341
  36.5 2.6 %collective-permute-start.12 = (f32[400,128]{1,0:T(8,128)S(1)}, f32[400,128]{1,0:T(8,128)S(1)}, u32[]{:S(2)}, u32[]{:S(2)}) collective-permute-start(f32[400,128]{1,0:T(8,128)S(1)} %add_terms.16), channel_id=1, source_target_pairs={{0,8},{1,9},{2,10},{3,11},{4,12},{5,13},{6,14},{7,15},{8,0},{9,1},... | collective-permute-start | bytes 614408 | tf_op jit(solution)/shard_map/ppermute | solution.py:341
  39.2 0.4 collective-permute-start.6
  39.6 13.1 %collective-permute-done.6.refs_3_.refs_6_ = f32[256,128]{1,0:T(8,128)S(1)} collective-permute-done((f32[256,128]{1,0:T(8,128)S(1)}, f32[256,128]{1,0:T(8,128)S(1)}, u32[]{:S(2)}, u32[]{:S(2)}) %collective-permute-start.6) | collective-permute-done | bytes 131104 | tf_op jit(solution)/shard_map/ppermute | solution.py:341
  52.7 1.5 %collective-permute-start.15 = (f32[128,128]{1,0:T(8,128)S(1)}, f32[128,128]{1,0:T(8,128)S(1)}, u32[]{:S(2)}, u32[]{:S(2)}) collective-permute-start(f32[128,128]{1,0:T(8,128)S(1)} %add_terms.19), channel_id=1, source_target_pairs={{0,2},{1,3},{2,0},{3,1},{4,6},{5,7},{6,4},{7,5},{8,10},{9,11},{10,... | collective-permute-start | bytes 196616 | tf_op jit(solution)/shard_map/ppermute | solution.py:341
  54.3 1.6 %tile_index.1.index_ref = s32[48]{0:T(128)S(1)} custom-call(s32[256]{0:T(256)S(1)} %copy-done), custom_call_target="tpu_custom_call" | custom-call | flops 1000000 | bytes 1024 | tf_op jit(solution)/shard_map/tile_index/pallas_call | solution.py:232
  55.9 1.2 %collective-permute-done.15.refs_9_ = f32[128,128]{1,0:T(8,128)S(1)} collective-permute-done((f32[128,128]{1,0:T(8,128)S(1)}, f32[128,128]{1,0:T(8,128)S(1)}, u32[]{:S(2)}, u32[]{:S(2)}) %collective-permute-start.15) | collective-permute-done | bytes 65568 | tf_op jit(solution)/shard_map/ppermute | solution.py:341
  57.1 1.9 %finish_tiles.1 = f32[16,4096]{1,0:T(8,128)} custom-call(s32[48]{0:T(128)S(1)} %tile_index.1.index_ref, f32[512,128]{1,0:T(8,128)S(1)} %get-tuple-element.21.refs_0_, f32[1600,128]{1,0:T(8,128)S(1)} %get-tuple-element.22.refs_0_.refs_1_, f32[512,128]{1,0:T(8,128)S(1)} %collective-permute-done.1.refs_1_.refs_2_, ...), custom_call_target="tpu_custom_call" | custom-call | flops 540672 | bytes 2162688 | tf_op jit(solution)/shard_map/finish_tiles/pallas_call | solution.py:174
  (25 shorter events, 0.5 us)
Async XLA Ops:
  0.0 12.6 %copy-start = (s32[256]{0:T(256)S(1)}, s32[256]{0:T(256)}, u32[]{:S(2)}) copy-start(s32[256]{0:T(256)} %owner_ref.5) | copy-start | bytes 3076
  13.3 14.3 %collective-permute-start.3 = (f32[1600,128]{1,0:T(8,128)S(1)}, f32[1600,128]{1,0:T(8,128)S(1)}, u32[]{:S(2)}, u32[]{:S(2)}) collective-permute-start(f32[1600,128]{1,0:T(8,128)S(1)} %get-tuple-element.26), channel_id=1, source_target_pairs={{0,1},{1,0},{2,3},{3,2},{4,5},{5,4},{6,7},{7,6},{8,9},{9,8},{10,11... | collective-permute-start | bytes 2457608 | tf_op jit(solution)/shard_map/ppermute | solution.py:341
  13.9 7.5 %collective-permute-start.4 = (f32[800,128]{1,0:T(8,128)S(1)}, f32[800,128]{1,0:T(8,128)S(1)}, u32[]{:S(2)}, u32[]{:S(2)}) collective-permute-start(f32[800,128]{1,0:T(8,128)S(1)} %get-tuple-element.28), channel_id=1, source_target_pairs={{0,1},{1,0},{2,3},{3,2},{4,5},{5,4},{6,7},{7,6},{8,9},{9,8},{10,11... | collective-permute-start | bytes 1228808 | tf_op jit(solution)/shard_map/ppermute | solution.py:341
  14.0 2.8 %collective-permute-start.9 = (f32[400,128]{1,0:T(8,128)S(1)}, f32[400,128]{1,0:T(8,128)S(1)}, u32[]{:S(2)}, u32[]{:S(2)}) collective-permute-start(f32[400,128]{1,0:T(8,128)S(1)} %get-tuple-element.32), channel_id=1, source_target_pairs={{0,1},{1,0},{2,3},{3,2},{4,5},{5,4},{6,7},{7,6},{8,9},{9,8},{10,11... | collective-permute-start | bytes 614408 | tf_op jit(solution)/shard_map/ppermute | solution.py:341
  14.4 5.3 %collective-permute-start = (f32[512,128]{1,0:T(8,128)S(1)}, f32[512,128]{1,0:T(8,128)S(1)}, u32[]{:S(2)}, u32[]{:S(2)}) collective-permute-start(f32[512,128]{1,0:T(8,128)S(1)} %get-tuple-element.24), channel_id=1, source_target_pairs={{0,1},{1,0},{2,3},{3,2},{4,5},{5,4},{6,7},{7,6},{8,9},{9,8},{10,11... | collective-permute-start | bytes 786440 | tf_op jit(solution)/shard_map/ppermute | solution.py:341
  14.5 5.2 %collective-permute-start.7 = (f32[400,128]{1,0:T(8,128)S(1)}, f32[400,128]{1,0:T(8,128)S(1)}, u32[]{:S(2)}, u32[]{:S(2)}) collective-permute-start(f32[400,128]{1,0:T(8,128)S(1)} %get-tuple-element.30), channel_id=1, source_target_pairs={{0,1},{1,0},{2,3},{3,2},{4,5},{5,4},{6,7},{7,6},{8,9},{9,8},{10,11... | collective-permute-start | bytes 614408 | tf_op jit(solution)/shard_map/ppermute | solution.py:341
  16.8 8.8 %collective-permute-start.10 = (f32[400,128]{1,0:T(8,128)S(1)}, f32[400,128]{1,0:T(8,128)S(1)}, u32[]{:S(2)}, u32[]{:S(2)}) collective-permute-start(f32[400,128]{1,0:T(8,128)S(1)} %add_terms.14), channel_id=1, source_target_pairs={{0,2},{1,3},{2,0},{3,1},{4,6},{5,7},{6,4},{7,5},{8,10},{9,11},{10,... | collective-permute-start | bytes 614408 | tf_op jit(solution)/shard_map/ppermute | solution.py:341
  19.7 19.5 %collective-permute-start.2 = (f32[512,128]{1,0:T(8,128)S(1)}, f32[512,128]{1,0:T(8,128)S(1)}, u32[]{:S(2)}, u32[]{:S(2)}) collective-permute-start(f32[512,128]{1,0:T(8,128)S(1)} %get-tuple-element.25), channel_id=1, source_target_pairs={{0,1},{1,0},{2,3},{3,2},{4,5},{5,4},{6,7},{7,6},{8,9},{9,8},{10,11... | collective-permute-start | bytes 786440 | tf_op jit(solution)/shard_map/ppermute | solution.py:341
  19.7 19.5 %collective-permute-start.1 = (f32[512,128]{1,0:T(8,128)S(1)}, f32[512,128]{1,0:T(8,128)S(1)}, u32[]{:S(2)}, u32[]{:S(2)}) collective-permute-start(f32[512,128]{1,0:T(8,128)S(1)} %add_terms.10), channel_id=1, source_target_pairs={{0,4},{1,5},{2,6},{3,7},{4,0},{5,1},{6,2},{7,3},{8,12},{9,13},{10,... | collective-permute-start | bytes 786440 | tf_op jit(solution)/shard_map/ppermute | solution.py:341
  21.4 8.5 %collective-permute-start.13 = (f32[400,128]{1,0:T(8,128)S(1)}, f32[400,128]{1,0:T(8,128)S(1)}, u32[]{:S(2)}, u32[]{:S(2)}) collective-permute-start(f32[400,128]{1,0:T(8,128)S(1)} %add_terms.17), channel_id=1, source_target_pairs={{0,2},{1,3},{2,0},{3,1},{4,6},{5,7},{6,4},{7,5},{8,10},{9,11},{10,... | collective-permute-start | bytes 614408 | tf_op jit(solution)/shard_map/ppermute | solution.py:341
  25.6 8.8 %collective-permute-start.8 = (f32[400,128]{1,0:T(8,128)S(1)}, f32[400,128]{1,0:T(8,128)S(1)}, u32[]{:S(2)}, u32[]{:S(2)}) collective-permute-start(f32[400,128]{1,0:T(8,128)S(1)} %add_terms.13), channel_id=1, source_target_pairs={{0,2},{1,3},{2,0},{3,1},{4,6},{5,7},{6,4},{7,5},{8,10},{9,11},{10,... | collective-permute-start | bytes 614408 | tf_op jit(solution)/shard_map/ppermute | solution.py:341
  27.7 8.8 %collective-permute-start.11 = (f32[400,128]{1,0:T(8,128)S(1)}, f32[400,128]{1,0:T(8,128)S(1)}, u32[]{:S(2)}, u32[]{:S(2)}) collective-permute-start(f32[400,128]{1,0:T(8,128)S(1)} %add_terms.15), channel_id=1, source_target_pairs={{0,4},{1,5},{2,6},{3,7},{4,0},{5,1},{6,2},{7,3},{8,12},{9,13},{10,... | collective-permute-start | bytes 614408 | tf_op jit(solution)/shard_map/ppermute | solution.py:341
  30.0 25.9 %collective-permute-start.5 = (f32[400,128]{1,0:T(8,128)S(1)}, f32[400,128]{1,0:T(8,128)S(1)}, u32[]{:S(2)}, u32[]{:S(2)}) collective-permute-start(f32[400,128]{1,0:T(8,128)S(1)} %add_terms.11), channel_id=1, source_target_pairs={{0,2},{1,3},{2,0},{3,1},{4,6},{5,7},{6,4},{7,5},{8,10},{9,11},{10,... | collective-permute-start | bytes 614408 | tf_op jit(solution)/shard_map/ppermute | solution.py:341
  34.4 22.7 %collective-permute-start.14 = (f32[400,128]{1,0:T(8,128)S(1)}, f32[400,128]{1,0:T(8,128)S(1)}, u32[]{:S(2)}, u32[]{:S(2)}) collective-permute-start(f32[400,128]{1,0:T(8,128)S(1)} %add_terms.18), channel_id=1, source_target_pairs={{0,4},{1,5},{2,6},{3,7},{4,0},{5,1},{6,2},{7,3},{8,12},{9,13},{10,... | collective-permute-start | bytes 614408 | tf_op jit(solution)/shard_map/ppermute | solution.py:341
  36.5 20.5 %collective-permute-start.12 = (f32[400,128]{1,0:T(8,128)S(1)}, f32[400,128]{1,0:T(8,128)S(1)}, u32[]{:S(2)}, u32[]{:S(2)}) collective-permute-start(f32[400,128]{1,0:T(8,128)S(1)} %add_terms.16), channel_id=1, source_target_pairs={{0,8},{1,9},{2,10},{3,11},{4,12},{5,13},{6,14},{7,15},{8,0},{9,1},... | collective-permute-start | bytes 614408 | tf_op jit(solution)/shard_map/ppermute | solution.py:341
  39.2 13.5 %collective-permute-start.6 = (f32[256,128]{1,0:T(8,128)S(1)}, f32[256,128]{1,0:T(8,128)S(1)}, u32[]{:S(2)}, u32[]{:S(2)}) collective-permute-start(f32[256,128]{1,0:T(8,128)S(1)} %add_terms.12), channel_id=1, source_target_pairs={{0,8},{1,9},{2,10},{3,11},{4,12},{5,13},{6,14},{7,15},{8,0},{9,1},... | collective-permute-start | bytes 393224 | tf_op jit(solution)/shard_map/ppermute | solution.py:341
  52.7 4.3 %collective-permute-start.15 = (f32[128,128]{1,0:T(8,128)S(1)}, f32[128,128]{1,0:T(8,128)S(1)}, u32[]{:S(2)}, u32[]{:S(2)}) collective-permute-start(f32[128,128]{1,0:T(8,128)S(1)} %add_terms.19), channel_id=1, source_target_pairs={{0,2},{1,3},{2,0},{3,1},{4,6},{5,7},{6,4},{7,5},{8,10},{9,11},{10,... | collective-permute-start | bytes 196616 | tf_op jit(solution)/shard_map/ppermute | solution.py:341
where the time goes:
time: 59.1 us; the launch traced here: 58.9 us
  waiting for transfers between devices  21.9 us (37%)
  starting transfers between devices  19.1 us (32%)
  Pallas kernels  17.8 us (30%)
    ppermute x16, waiting for transfers between devices, shards(): arrays.append(lax.ppermute(sent, AXES, pairs(axis, bit)))  21.9 us
    ppermute x16, starting transfers between devices, shards(): arrays.append(lax.ppermute(sent, AXES, pairs(axis, bit)))  19.1 us
    pallas_call x1, Pallas kernels, gram_tiles(): pl.pallas_call(functools.partial(gram_kernel, cuts, spans), out_shape=[ja...  12.6 us
    pallas_call x1, Pallas kernels, finish(): pl.pallas_call(functools.partial(finish_kernel, joined, slots, features),...  1.87 us
    pallas_call x1, Pallas kernels, tile_index(): pl.pallas_call(functools.partial(index_kernel, slots, columns, firsts), o...  1.61 us
    pallas_call x2, Pallas kernels, pick_tiles(): pl.pallas_call(functools.partial(pick_kernel, pieces, bounds, columns, sl...  1.43 us
  transfers between devices with their start and end apart: 16, of which 6 were waited for; matrix products, arithmetic and copies ran while one was open for 0% of the time, Pallas kernels for 5%

commit v1 on v0

--- a/solution.py
+++ b/solution.py
@@ -126,8 +126,8 @@
 
 
 def finish_kernel(joined, slots, features, index_ref, *refs):
-    out_ref, total, inv, rows_of, cols_of, packed = refs[-6:]
-    add_kernel(joined, *refs[:-6], total)
+    out_hbm, total, inv, rows_of, cols_of, packed, out_ref, sems = refs[-8:]
+    add_kernel(joined, *refs[:-8], total)
     meansq = total[slots * HALF :, :] / features + EPS
     inv[...] = 1.0 / jnp.sqrt(meansq)
     half = lax.broadcasted_iota(jnp.int32, (1, LANES), 1) < TILE
@@ -155,6 +155,7 @@
         packed[i * PITCH : i * PITCH + HALF, :] = jnp.where(alive, scaled, 0.0)
     step = min(slots, 8)
     wide = lax.broadcasted_iota(jnp.int32, (step, LANES), 1) < TILE
+    copies = []
     for s in range(0, slots, step):
         for j in range(HALF):
             q = (2 * j) % HALF
@@ -165,6 +166,11 @@
             else:
                 line = jnp.where(wide, pltpu.roll(even, TILE, 1), odd)
             out_ref[s : s + step, j * LANES : (j + 1) * LANES] = line
+        copy = pltpu.make_async_copy(out_ref.at[pl.ds(s, step)], out_hbm.at[pl.ds(s, step)], sems.at[s // step])
+        copy.start()
+        copies.append(copy)
+    for copy in copies:
+        copy.wait()
 
 
 def finish(index, arrays, joined, slots, features):
@@ -175,13 +181,15 @@
         functools.partial(finish_kernel, joined, slots, features),
         out_shape=jax.ShapeDtypeStruct((slots, TILE * TILE), jnp.float32),
         in_specs=[pl.BlockSpec(memory_space=pltpu.SMEM)] + [vmem] * len(arrays),
-        out_specs=vmem,
+        out_specs=pl.BlockSpec(memory_space=pltpu.HBM),
         scratch_shapes=[
             pltpu.VMEM((per, LANES), jnp.float32),
             pltpu.VMEM((extra, LANES), jnp.float32),
             pltpu.VMEM((LANES, LANES), jnp.float32),
             pltpu.VMEM((max(slots, 8), LANES), jnp.float32),
             pltpu.VMEM((slots * PITCH, LANES), jnp.float32),
+            pltpu.VMEM((slots, TILE * TILE), jnp.float32),
+            pltpu.SemaphoreType.DMA((-(-slots // 8),)),
         ],
         compiler_params=pltpu.CompilerParams(vmem_limit_bytes=6 * 2**20),
         cost_estimate=pl.CostEstimate(flops=per * LANES * 8, bytes_accessed=per * LANES * 32, transcendentals=0),

time: 59.1 us -> 59.1 us (level)
  no operation moved by 1% of the time
where the time goes in v1:
time: 59.1 us; the launch traced here: 58.9 us
  waiting for transfers between devices  21.9 us (37%)
  starting transfers between devices  19.1 us (32%)
  Pallas kernels  17.8 us (30%)
    ppermute x16, waiting for transfers between devices, shards(): arrays.append(lax.ppermute(sent, AXES, pairs(axis, bit)))  21.9 us
    ppermute x16, starting transfers between devices, shards(): arrays.append(lax.ppermute(sent, AXES, pairs(axis, bit)))  19.1 us
    pallas_call x1, Pallas kernels, gram_tiles(): pl.pallas_call(functools.partial(gram_kernel, cuts, spans), out_shape=[ja...  12.6 us
    pallas_call x1, Pallas kernels, finish(): pl.pallas_call(functools.partial(finish_kernel, joined, slots, features),...  1.85 us
    pallas_call x1, Pallas kernels, tile_index(): pl.pallas_call(functools.partial(index_kernel, slots, columns, firsts), o...  1.61 us
    pallas_call x2, Pallas kernels, pick_tiles(): pl.pallas_call(functools.partial(pick_kernel, pieces, bounds, columns, sl...  1.43 us
  transfers between devices with their start and end apart: 16, of which 6 were waited for; matrix products, arithmetic and copies ran while one was open for 0% of the time, Pallas kernels for 5%

profile of v1, /device:TPU:0, one launch (start us, length us, event | category | flops | bytes accessed | tf_op | source)
XLA Modules:
  0.0 58.9 jit_solution(9231588629702070930)
XLA Ops:
  0.0 12.6 %gram_tiles.1 = (f32[8192,128]{1,0:T(8,128)S(1)}, f32[16,128]{1,0:T(8,128)S(1)}) custom-call(bf16[1408,4096]{1,0:T(8,128)(2,1)} %hbm_ref.1), custom_call_target="tpu_custom_call" | custom-call | flops 8120172544 | bytes 15728640 | tf_op jit(solution)/shard_map/gram_tiles/pallas_call | solution.py:77
  12.6 0.7 %pick_tiles.3 = (f32[400,128]{1,0:T(8,128)S(1)}, f32[512,128]{1,0:T(8,128)S(1)}, f32[400,128]{1,0:T(8,128)S(1)}, f32[800,128]{1,0:T(8,128)S(1)}, f32[512,128]{1,0:T(8,128)S(1)}, /*index=5*/f32[1600,128]{1,0:T(8,128)S(1)}) custom-call(s32[256]{0:T(256)S(1)} %copy-done, f32[8192,128]{1,0:T(8,128)S(1)} %get-tuple-element.19.tiles, ...), custom_call_target="tpu_custom_call" | custom-call | flops 1000000 | bytes 4325376 | tf_op jit(solution)/shard_map/pick_tiles/pallas_call | solution.py:117
  13.3 0.6 collective-permute-start.3
  14.0 0.4 collective-permute-start.9
  14.5 0.4 collective-permute-start.7
  14.9 0.7 %pick_tiles.2 = (f32[400,128]{1,0:T(8,128)S(1)}, f32[512,128]{1,0:T(8,128)S(1)}, f32[400,128]{1,0:T(8,128)S(1)}, f32[800,128]{1,0:T(8,128)S(1)}, f32[512,128]{1,0:T(8,128)S(1)}, /*index=5*/f32[1600,128]{1,0:T(8,128)S(1)}) custom-call(s32[256]{0:T(256)S(1)} %copy-done, f32[8192,128]{1,0:T(8,128)S(1)} %get-tuple-element.19.tiles, ...), custom_call_target="tpu_custom_call" | custom-call | flops 1000000 | bytes 4325376 | tf_op jit(solution)/shard_map/pick_tiles/pallas_call | solution.py:117
  15.6 1.1 %collective-permute-done.9.refs_1_ = f32[400,128]{1,0:T(8,128)S(1)} collective-permute-done((f32[400,128]{1,0:T(8,128)S(1)}, f32[400,128]{1,0:T(8,128)S(1)}, u32[]{:S(2)}, u32[]{:S(2)}) %collective-permute-start.9) | collective-permute-done | bytes 204832 | tf_op jit(solution)/shard_map/ppermute | solution.py:349
  16.8 2.9 %collective-permute-start.10 = (f32[400,128]{1,0:T(8,128)S(1)}, f32[400,128]{1,0:T(8,128)S(1)}, u32[]{:S(2)}, u32[]{:S(2)}) collective-permute-start(f32[400,128]{1,0:T(8,128)S(1)} %add_terms.14), channel_id=1, source_target_pairs={{0,2},{1,3},{2,0},{3,1},{4,6},{5,7},{6,4},{7,5},{8,10},{9,11},{10,... | collective-permute-start | bytes 614408 | tf_op jit(solution)/shard_map/ppermute | solution.py:349
  19.7 1.6 %collective-permute-start.1 = (f32[512,128]{1,0:T(8,128)S(1)}, f32[512,128]{1,0:T(8,128)S(1)}, u32[]{:S(2)}, u32[]{:S(2)}) collective-permute-start(f32[512,128]{1,0:T(8,128)S(1)} %add_terms.10), channel_id=1, source_target_pairs={{0,4},{1,5},{2,6},{3,7},{4,0},{5,1},{6,2},{7,3},{8,12},{9,13},{10,... | collective-permute-start | bytes 786440 | tf_op jit(solution)/shard_map/ppermute | solution.py:349
  21.4 0.6 %collective-permute-start.13 = (f32[400,128]{1,0:T(8,128)S(1)}, f32[400,128]{1,0:T(8,128)S(1)}, u32[]{:S(2)}, u32[]{:S(2)}) collective-permute-start(f32[400,128]{1,0:T(8,128)S(1)} %add_terms.17), channel_id=1, source_target_pairs={{0,2},{1,3},{2,0},{3,1},{4,6},{5,7},{6,4},{7,5},{8,10},{9,11},{10,... | collective-permute-start | bytes 614408 | tf_op jit(solution)/shard_map/ppermute | solution.py:349
  22.0 3.6 %collective-permute-done.10.refs_1_ = f32[400,128]{1,0:T(8,128)S(1)} collective-permute-done((f32[400,128]{1,0:T(8,128)S(1)}, f32[400,128]{1,0:T(8,128)S(1)}, u32[]{:S(2)}, u32[]{:S(2)}) %collective-permute-start.10) | collective-permute-done | bytes 204832 | tf_op jit(solution)/shard_map/ppermute | solution.py:349
  25.6 2.0 %collective-permute-start.8 = (f32[400,128]{1,0:T(8,128)S(1)}, f32[400,128]{1,0:T(8,128)S(1)}, u32[]{:S(2)}, u32[]{:S(2)}) collective-permute-start(f32[400,128]{1,0:T(8,128)S(1)} %add_terms.13), channel_id=1, source_target_pairs={{0,2},{1,3},{2,0},{3,1},{4,6},{5,7},{6,4},{7,5},{8,10},{9,11},{10,... | collective-permute-start | bytes 614408 | tf_op jit(solution)/shard_map/ppermute | solution.py:349
  27.7 1.6 %collective-permute-start.11 = (f32[400,128]{1,0:T(8,128)S(1)}, f32[400,128]{1,0:T(8,128)S(1)}, u32[]{:S(2)}, u32[]{:S(2)}) collective-permute-start(f32[400,128]{1,0:T(8,128)S(1)} %add_terms.15), channel_id=1, source_target_pairs={{0,4},{1,5},{2,6},{3,7},{4,0},{5,1},{6,2},{7,3},{8,12},{9,13},{10,... | collective-permute-start | bytes 614408 | tf_op jit(solution)/shard_map/ppermute | solution.py:349
  29.3 0.6 %collective-permute-done.13.refs_2_ = f32[400,128]{1,0:T(8,128)S(1)} collective-permute-done((f32[400,128]{1,0:T(8,128)S(1)}, f32[400,128]{1,0:T(8,128)S(1)}, u32[]{:S(2)}, u32[]{:S(2)}) %collective-permute-start.13) | collective-permute-done | bytes 204832 | tf_op jit(solution)/shard_map/ppermute | solution.py:349
  30.0 2.0 %collective-permute-start.5 = (f32[400,128]{1,0:T(8,128)S(1)}, f32[400,128]{1,0:T(8,128)S(1)}, u32[]{:S(2)}, u32[]{:S(2)}) collective-permute-start(f32[400,128]{1,0:T(8,128)S(1)} %add_terms.11), channel_id=1, source_target_pairs={{0,2},{1,3},{2,0},{3,1},{4,6},{5,7},{6,4},{7,5},{8,10},{9,11},{10,... | collective-permute-start | bytes 614408 | tf_op jit(solution)/shard_map/ppermute | solution.py:349
  32.0 2.3 %collective-permute-done.8.refs_2_ = f32[400,128]{1,0:T(8,128)S(1)} collective-permute-done((f32[400,128]{1,0:T(8,128)S(1)}, f32[400,128]{1,0:T(8,128)S(1)}, u32[]{:S(2)}, u32[]{:S(2)}) %collective-permute-start.8) | collective-permute-done | bytes 204832 | tf_op jit(solution)/shard_map/ppermute | solution.py:349
  34.4 2.1 %collective-permute-start.14 = (f32[400,128]{1,0:T(8,128)S(1)}, f32[400,128]{1,0:T(8,128)S(1)}, u32[]{:S(2)}, u32[]{:S(2)}) collective-permute-start(f32[400,128]{1,0:T(8,128)S(1)} %add_terms.18), channel_id=1, source_target_pairs={{0,4},{1,5},{2,6},{3,7},{4,0},{5,1},{6,2},{7,3},{8,12},{9,13},{10,... | collective-permute-start | bytes 614408 | tf_op jit(solution)/shard_map/ppermute | solution.py:349
  36.5 2.6 %collective-permute-start.12 = (f32[400,128]{1,0:T(8,128)S(1)}, f32[400,128]{1,0:T(8,128)S(1)}, u32[]{:S(2)}, u32[]{:S(2)}) collective-permute-start(f32[400,128]{1,0:T(8,128)S(1)} %add_terms.16), channel_id=1, source_target_pairs={{0,8},{1,9},{2,10},{3,11},{4,12},{5,13},{6,14},{7,15},{8,0},{9,1},... | collective-permute-start | bytes 614408 | tf_op jit(solution)/shard_map/ppermute | solution.py:349
  39.2 0.4 collective-permute-start.6
  39.6 13.1 %collective-permute-done.6.refs_3_.refs_6_ = f32[256,128]{1,0:T(8,128)S(1)} collective-permute-done((f32[256,128]{1,0:T(8,128)S(1)}, f32[256,128]{1,0:T(8,128)S(1)}, u32[]{:S(2)}, u32[]{:S(2)}) %collective-permute-start.6) | collective-permute-done | bytes 131104 | tf_op jit(solution)/shard_map/ppermute | solution.py:349
  52.7 1.5 %collective-permute-start.15 = (f32[128,128]{1,0:T(8,128)S(1)}, f32[128,128]{1,0:T(8,128)S(1)}, u32[]{:S(2)}, u32[]{:S(2)}) collective-permute-start(f32[128,128]{1,0:T(8,128)S(1)} %add_terms.19), channel_id=1, source_target_pairs={{0,2},{1,3},{2,0},{3,1},{4,6},{5,7},{6,4},{7,5},{8,10},{9,11},{10,... | collective-permute-start | bytes 196616 | tf_op jit(solution)/shard_map/ppermute | solution.py:349
  54.3 1.6 %tile_index.1.index_ref = s32[48]{0:T(128)S(1)} custom-call(s32[256]{0:T(256)S(1)} %copy-done), custom_call_target="tpu_custom_call" | custom-call | flops 1000000 | bytes 1024 | tf_op jit(solution)/shard_map/tile_index/pallas_call | solution.py:240
  55.9 1.2 %collective-permute-done.15.refs_9_ = f32[128,128]{1,0:T(8,128)S(1)} collective-permute-done((f32[128,128]{1,0:T(8,128)S(1)}, f32[128,128]{1,0:T(8,128)S(1)}, u32[]{:S(2)}, u32[]{:S(2)}) %collective-permute-start.15) | collective-permute-done | bytes 65568 | tf_op jit(solution)/shard_map/ppermute | solution.py:349
  57.1 1.9 %finish_tiles.1 = f32[16,4096]{1,0:T(8,128)} custom-call(s32[48]{0:T(128)S(1)} %tile_index.1.index_ref, f32[512,128]{1,0:T(8,128)S(1)} %get-tuple-element.21.refs_0_, f32[1600,128]{1,0:T(8,128)S(1)} %get-tuple-element.22.refs_0_.refs_1_, f32[512,128]{1,0:T(8,128)S(1)} %collective-permute-done.1.refs_1_.refs_2_, ...), custom_call_target="tpu_custom_call" | custom-call | flops 540672 | bytes 2162688 | tf_op jit(solution)/shard_map/finish_tiles/pallas_call | solution.py:180
  (25 shorter events, 0.5 us)
Async XLA Ops:
  0.0 12.6 %copy-start = (s32[256]{0:T(256)S(1)}, s32[256]{0:T(256)}, u32[]{:S(2)}) copy-start(s32[256]{0:T(256)} %owner_ref.5) | copy-start | bytes 3076
  13.3 14.3 %collective-permute-start.3 = (f32[1600,128]{1,0:T(8,128)S(1)}, f32[1600,128]{1,0:T(8,128)S(1)}, u32[]{:S(2)}, u32[]{:S(2)}) collective-permute-start(f32[1600,128]{1,0:T(8,128)S(1)} %get-tuple-element.26), channel_id=1, source_target_pairs={{0,1},{1,0},{2,3},{3,2},{4,5},{5,4},{6,7},{7,6},{8,9},{9,8},{10,11... | collective-permute-start | bytes 2457608 | tf_op jit(solution)/shard_map/ppermute | solution.py:349
  13.9 7.5 %collective-permute-start.4 = (f32[800,128]{1,0:T(8,128)S(1)}, f32[800,128]{1,0:T(8,128)S(1)}, u32[]{:S(2)}, u32[]{:S(2)}) collective-permute-start(f32[800,128]{1,0:T(8,128)S(1)} %get-tuple-element.28), channel_id=1, source_target_pairs={{0,1},{1,0},{2,3},{3,2},{4,5},{5,4},{6,7},{7,6},{8,9},{9,8},{10,11... | collective-permute-start | bytes 1228808 | tf_op jit(solution)/shard_map/ppermute | solution.py:349
  14.0 2.8 %collective-permute-start.9 = (f32[400,128]{1,0:T(8,128)S(1)}, f32[400,128]{1,0:T(8,128)S(1)}, u32[]{:S(2)}, u32[]{:S(2)}) collective-permute-start(f32[400,128]{1,0:T(8,128)S(1)} %get-tuple-element.32), channel_id=1, source_target_pairs={{0,1},{1,0},{2,3},{3,2},{4,5},{5,4},{6,7},{7,6},{8,9},{9,8},{10,11... | collective-permute-start | bytes 614408 | tf_op jit(solution)/shard_map/ppermute | solution.py:349
  14.4 5.3 %collective-permute-start = (f32[512,128]{1,0:T(8,128)S(1)}, f32[512,128]{1,0:T(8,128)S(1)}, u32[]{:S(2)}, u32[]{:S(2)}) collective-permute-start(f32[512,128]{1,0:T(8,128)S(1)} %get-tuple-element.24), channel_id=1, source_target_pairs={{0,1},{1,0},{2,3},{3,2},{4,5},{5,4},{6,7},{7,6},{8,9},{9,8},{10,11... | collective-permute-start | bytes 786440 | tf_op jit(solution)/shard_map/ppermute | solution.py:349
  14.5 5.2 %collective-permute-start.7 = (f32[400,128]{1,0:T(8,128)S(1)}, f32[400,128]{1,0:T(8,128)S(1)}, u32[]{:S(2)}, u32[]{:S(2)}) collective-permute-start(f32[400,128]{1,0:T(8,128)S(1)} %get-tuple-element.30), channel_id=1, source_target_pairs={{0,1},{1,0},{2,3},{3,2},{4,5},{5,4},{6,7},{7,6},{8,9},{9,8},{10,11... | collective-permute-start | bytes 614408 | tf_op jit(solution)/shard_map/ppermute | solution.py:349
  16.8 8.8 %collective-permute-start.10 = (f32[400,128]{1,0:T(8,128)S(1)}, f32[400,128]{1,0:T(8,128)S(1)}, u32[]{:S(2)}, u32[]{:S(2)}) collective-permute-start(f32[400,128]{1,0:T(8,128)S(1)} %add_terms.14), channel_id=1, source_target_pairs={{0,2},{1,3},{2,0},{3,1},{4,6},{5,7},{6,4},{7,5},{8,10},{9,11},{10,... | collective-permute-start | bytes 614408 | tf_op jit(solution)/shard_map/ppermute | solution.py:349
  19.7 19.5 %collective-permute-start.2 = (f32[512,128]{1,0:T(8,128)S(1)}, f32[512,128]{1,0:T(8,128)S(1)}, u32[]{:S(2)}, u32[]{:S(2)}) collective-permute-start(f32[512,128]{1,0:T(8,128)S(1)} %get-tuple-element.25), channel_id=1, source_target_pairs={{0,1},{1,0},{2,3},{3,2},{4,5},{5,4},{6,7},{7,6},{8,9},{9,8},{10,11... | collective-permute-start | bytes 786440 | tf_op jit(solution)/shard_map/ppermute | solution.py:349
  19.7 19.5 %collective-permute-start.1 = (f32[512,128]{1,0:T(8,128)S(1)}, f32[512,128]{1,0:T(8,128)S(1)}, u32[]{:S(2)}, u32[]{:S(2)}) collective-permute-start(f32[512,128]{1,0:T(8,128)S(1)} %add_terms.10), channel_id=1, source_target_pairs={{0,4},{1,5},{2,6},{3,7},{4,0},{5,1},{6,2},{7,3},{8,12},{9,13},{10,... | collective-permute-start | bytes 786440 | tf_op jit(solution)/shard_map/ppermute | solution.py:349
  21.4 8.5 %collective-permute-start.13 = (f32[400,128]{1,0:T(8,128)S(1)}, f32[400,128]{1,0:T(8,128)S(1)}, u32[]{:S(2)}, u32[]{:S(2)}) collective-permute-start(f32[400,128]{1,0:T(8,128)S(1)} %add_terms.17), channel_id=1, source_target_pairs={{0,2},{1,3},{2,0},{3,1},{4,6},{5,7},{6,4},{7,5},{8,10},{9,11},{10,... | collective-permute-start | bytes 614408 | tf_op jit(solution)/shard_map/ppermute | solution.py:349
  25.6 8.8 %collective-permute-start.8 = (f32[400,128]{1,0:T(8,128)S(1)}, f32[400,128]{1,0:T(8,128)S(1)}, u32[]{:S(2)}, u32[]{:S(2)}) collective-permute-start(f32[400,128]{1,0:T(8,128)S(1)} %add_terms.13), channel_id=1, source_target_pairs={{0,2},{1,3},{2,0},{3,1},{4,6},{5,7},{6,4},{7,5},{8,10},{9,11},{10,... | collective-permute-start | bytes 614408 | tf_op jit(solution)/shard_map/ppermute | solution.py:349
  27.7 8.8 %collective-permute-start.11 = (f32[400,128]{1,0:T(8,128)S(1)}, f32[400,128]{1,0:T(8,128)S(1)}, u32[]{:S(2)}, u32[]{:S(2)}) collective-permute-start(f32[400,128]{1,0:T(8,128)S(1)} %add_terms.15), channel_id=1, source_target_pairs={{0,4},{1,5},{2,6},{3,7},{4,0},{5,1},{6,2},{7,3},{8,12},{9,13},{10,... | collective-permute-start | bytes 614408 | tf_op jit(solution)/shard_map/ppermute | solution.py:349
  30.0 25.9 %collective-permute-start.5 = (f32[400,128]{1,0:T(8,128)S(1)}, f32[400,128]{1,0:T(8,128)S(1)}, u32[]{:S(2)}, u32[]{:S(2)}) collective-permute-start(f32[400,128]{1,0:T(8,128)S(1)} %add_terms.11), channel_id=1, source_target_pairs={{0,2},{1,3},{2,0},{3,1},{4,6},{5,7},{6,4},{7,5},{8,10},{9,11},{10,... | collective-permute-start | bytes 614408 | tf_op jit(solution)/shard_map/ppermute | solution.py:349
  34.4 22.7 %collective-permute-start.14 = (f32[400,128]{1,0:T(8,128)S(1)}, f32[400,128]{1,0:T(8,128)S(1)}, u32[]{:S(2)}, u32[]{:S(2)}) collective-permute-start(f32[400,128]{1,0:T(8,128)S(1)} %add_terms.18), channel_id=1, source_target_pairs={{0,4},{1,5},{2,6},{3,7},{4,0},{5,1},{6,2},{7,3},{8,12},{9,13},{10,... | collective-permute-start | bytes 614408 | tf_op jit(solution)/shard_map/ppermute | solution.py:349
  36.5 20.5 %collective-permute-start.12 = (f32[400,128]{1,0:T(8,128)S(1)}, f32[400,128]{1,0:T(8,128)S(1)}, u32[]{:S(2)}, u32[]{:S(2)}) collective-permute-start(f32[400,128]{1,0:T(8,128)S(1)} %add_terms.16), channel_id=1, source_target_pairs={{0,8},{1,9},{2,10},{3,11},{4,12},{5,13},{6,14},{7,15},{8,0},{9,1},... | collective-permute-start | bytes 614408 | tf_op jit(solution)/shard_map/ppermute | solution.py:349
  39.2 13.5 %collective-permute-start.6 = (f32[256,128]{1,0:T(8,128)S(1)}, f32[256,128]{1,0:T(8,128)S(1)}, u32[]{:S(2)}, u32[]{:S(2)}) collective-permute-start(f32[256,128]{1,0:T(8,128)S(1)} %add_terms.12), channel_id=1, source_target_pairs={{0,8},{1,9},{2,10},{3,11},{4,12},{5,13},{6,14},{7,15},{8,0},{9,1},... | collective-permute-start | bytes 393224 | tf_op jit(solution)/shard_map/ppermute | solution.py:349
  52.7 4.3 %collective-permute-start.15 = (f32[128,128]{1,0:T(8,128)S(1)}, f32[128,128]{1,0:T(8,128)S(1)}, u32[]{:S(2)}, u32[]{:S(2)}) collective-permute-start(f32[128,128]{1,0:T(8,128)S(1)} %add_terms.19), channel_id=1, source_target_pairs={{0,2},{1,3},{2,0},{3,1},{4,6},{5,7},{6,4},{7,5},{8,10},{9,11},{10,... | collective-permute-start | bytes 196616 | tf_op jit(solution)/shard_map/ppermute | solution.py:349
